TPU v7x, 512 devices: a whole 4x8x8 slice. The times are simulated.
512 devices in a mesh: dp: 16 (over z, core), fsdp: 32 (over x, y).
Axes of the slice: x: 4, y: 8, z: 8, core: 2. Of those that a mesh axis runs over, the one named last changes fastest.
Arguments:
- replica_grads: bfloat16 [16, 8192, 4096], P('dp', 'fsdp'), may hold values from -4 to 4
- slot_table: int32 [32], replicated, may hold values from 0 to 63, as said below
- left_gram_state: float32 [64, 4, 16, 16, 1024], P('fsdp', None, 'dp')
- right_gram_state: float32 [64, 4, 16, 16, 1024], P('fsdp', None, 'dp')
- left_inverse_root: bfloat16 [64, 4, 16, 16, 1024], P('fsdp', None, 'dp')
- right_inverse_root: bfloat16 [64, 4, 16, 16, 1024], P('fsdp', None, 'dp')
Outputs:
- direction: bfloat16 [32, 16, 16, 4096], P('fsdp', 'dp')
- left_new: float32 [64, 4, 16, 16, 1024], P('fsdp', None, 'dp')
- right_new: float32 [64, 4, 16, 16, 1024], P('fsdp', None, 'dp')
Inputs may be any that keep to these rules, and one draw needn't show every extreme that they name: `slot_table`: the entries are distinct; slot v belongs to owner v // 2 of the flat shards' devices; some owner holds 2 blocks.
All inputs are finite; a program needn't handle non-finite values.
Results may differ from a plain program's by a relative error of at most 0.02.
Values may be sent and summed in bfloat16 or wider, within the bound.
No kernel may reach another device: no remote copies, remote signals or barrier semaphores. Data moves between devices by JAX's collectives and lax.ppermute only.
A program may use at most 128 MiB of HBM per device.

v0:
```python
import jax
import jax.numpy as jnp
from jax import lax
from jax.sharding import PartitionSpec as P


def on_device(
    replica_grads,
    slot_table,
    left_gram_state,
    right_gram_state,
    left_inverse_root,
    right_inverse_root,
):
    slots_here = left_gram_state.shape[0]
    sub_blocks = left_gram_state.shape[1]
    strip_rows = left_gram_state.shape[3]
    block_size = left_gram_state.shape[4]
    band_rows = replica_grads.shape[1]
    model_width = replica_grads.shape[2]
    per_band = model_width // block_size
    shards = lax.axis_size("fsdp")
    groups = lax.axis_size("dp")
    total_slots = shards * slots_here
    block_count = slot_table.shape[0]
    band_index = lax.axis_index("fsdp")
    strip_index = lax.axis_index("dp")
    slot_indices = jnp.arange(total_slots, dtype=jnp.int32)
    right_entire = lax.all_gather(right_inverse_root, "dp", axis=2, tiled=True).reshape(
        slots_here, block_size, block_size
    )
    summed = lax.psum_scatter(
        replica_grads[0].astype(jnp.float32).astype(jnp.bfloat16),
        "dp",
        scatter_dimension=0,
        tiled=True,
    )
    row_block = band_index * band_rows // block_size
    targets = lax.dynamic_slice_in_dim(slot_table, row_block * per_band, per_band, 0)
    chooser = (targets[:, None] == slot_indices[None, :]).astype(jnp.bfloat16)
    own_slots = band_index * slots_here + jnp.arange(slots_here, dtype=jnp.int32)
    holder = slot_table[None, :] == own_slots[:, None]
    block_of = jnp.sum(
        jnp.where(holder, jnp.arange(block_count, dtype=jnp.int32)[None, :], 0), axis=1
    )
    first_band = block_of // per_band * sub_blocks
    outgoing = jnp.einsum(
        "cn,tcb->ntb",
        chooser,
        summed.reshape(strip_rows, per_band, block_size),
        preferred_element_type=jnp.float32,
    ).astype(jnp.bfloat16)
    outgoing = outgoing.reshape(shards, slots_here, strip_rows, block_size)
    arrived = lax.all_to_all(outgoing, "fsdp", split_axis=0, concat_axis=0, tiled=True)
    owned_rows = jax.vmap(
        lambda portion, offset: lax.dynamic_slice_in_dim(portion, offset, sub_blocks, 0),
        in_axes=(1, 0),
    )(arrived, first_band)
    owned_rows = owned_rows.reshape(slots_here, sub_blocks, 1, strip_rows, block_size)
    entire = lax.all_gather(owned_rows, "dp", axis=2, tiled=True).reshape(
        slots_here, block_size, block_size
    )
    my_rows = owned_rows.reshape(slots_here, sub_blocks * strip_rows, block_size)
    left_gram = jnp.einsum("mrc,mnc->mrn", my_rows, entire, preferred_element_type=jnp.float32)
    left_new = left_gram_state + (left_gram / block_size).reshape(left_gram_state.shape)
    my_columns = lax.dynamic_index_in_dim(
        entire.reshape(slots_here, block_size, sub_blocks, groups, strip_rows),
        strip_index,
        3,
        keepdims=False,
    )
    my_columns = my_columns.reshape(slots_here, block_size, sub_blocks * strip_rows)
    right_gram = jnp.einsum("mnr,mnc->mrc", my_columns, entire, preferred_element_type=jnp.float32)
    right_new = right_gram_state + (right_gram / block_size).reshape(right_gram_state.shape)
    left_rows = left_inverse_root.reshape(slots_here, sub_blocks * strip_rows, block_size)
    mixed_rows = jnp.einsum(
        "mrn,mnc->mrc", left_rows, entire, preferred_element_type=jnp.float32
    ).astype(jnp.bfloat16)
    result = jnp.einsum(
        "mrn,mnc->mrc", mixed_rows, right_entire, preferred_element_type=jnp.float32
    )
    outcome = result.astype(jnp.bfloat16).reshape(slots_here, sub_blocks, strip_rows, block_size)
    homeward = jax.vmap(
        lambda portion, offset: lax.dynamic_update_slice_in_dim(
            jnp.zeros((shards, strip_rows, block_size), jnp.bfloat16), portion, offset, 0
        ),
        out_axes=1,
    )(outcome, first_band)
    returned = lax.all_to_all(homeward, "fsdp", split_axis=0, concat_axis=0, tiled=True)
    picked = jnp.einsum(
        "cn,ntb->tcb",
        chooser,
        returned.reshape(total_slots, strip_rows, block_size),
        preferred_element_type=jnp.float32,
    ).astype(jnp.bfloat16)
    direction = picked.reshape(1, 1, strip_rows, model_width)
    return (direction, left_new, right_new)


def solution(mesh):
    placed = (
        P("dp", "fsdp", None),
        P(),
        P("fsdp", None, "dp", None, None),
        P("fsdp", None, "dp", None, None),
        P("fsdp", None, "dp", None, None),
        P("fsdp", None, "dp", None, None),
    )
    return jax.shard_map(
        on_device,
        mesh=mesh,
        in_specs=placed,
        out_specs=(
            P("fsdp", "dp", None, None),
            P("fsdp", None, "dp", None, None),
            P("fsdp", None, "dp", None, None),
        ),
        check_vma=False,
    )
```

profile of v0, /device:TPU:16, one launch (start us, length us, event | category | flops | bytes accessed | tf_op | source)
XLA Modules:
  0.0 276.2 jit_solution(1561728517146626942)
XLA Ops:
  7.2 0.7 reduce-scatter.2.cloned.1.call-update
  8.0 0.7 all-gather.4.cloned.1.call-update
  8.7 0.7 dynamic_slice.7
  9.4 69.5 %reduce-scatter.2.cloned.1.call-done = bf16[16,4096]{1,0:T(8,128)(2,1)} async-done(((bf16[256,4096]{1,0:T(8,128)(2,1)}), bf16[16,4096]{1,0:T(8,128)(2,1)}) %reduce-scatter.2.cloned.1.call-update) | async-done | bytes 131088 | tf_op jit(solution)/shard_map/reduce_scatter | solution.py:32
  78.9 1.0 reshape.110
  79.9 0.8 convolution_convert_fusion
  80.7 2.5 copy.35
  83.2 9.8 %all-to-all-start = ((bf16[32,2,16,1024]{3,2,1,0:T(8,128)(2,1)}), bf16[32,2,16,1024]{3,2,1,0:T(8,128)(2,1)S(1)}, u32[]{:S(2)}, u32[]{:S(2)}) async-start(bf16[32,2,16,1024]{3,2,1,0:T(8,128)(2,1)} %bitcast.3), calls=%async_computation.1 | async-start | bytes 4194304 | tf_op jit(solution)/shard_map/all_to_all | solution.py:54
  93.3 45.8 %all-to-all-done = bf16[32,2,16,1024]{3,2,1,0:T(8,128)(2,1)S(1)} async-done(((bf16[32,2,16,1024]{3,2,1,0:T(8,128)(2,1)}), bf16[32,2,16,1024]{3,2,1,0:T(8,128)(2,1)S(1)}, u32[]{:S(2)}, u32[]{:S(2)}) %all-to-all-start) | async-done | bytes 2097184 | tf_op jit(solution)/shard_map/all_to_all | solution.py:54
  139.1 1.3 gather_fusion
  140.6 42.7 %all-gather.6.cloned.1.call-done = bf16[2,4,256,1024]{3,2,1,0:T(8,128)(2,1)} async-done(((bf16[2,4,16,1024]{3,2,1,0:T(8,128)(2,1)}), bf16[2,4,256,1024]{3,2,1,0:T(8,128)(2,1)}) %all-gather.6.cloned.1.call-update) | async-done | bytes 4194320 | tf_op jit(solution)/shard_map/all_gather | solution.py:60
  183.4 5.1 %convolution_convert_fusion.2 = bf16[2,64,1024]{2,1,0:T(8,128)(2,1)S(1)} fusion(bf16[2,1024,1024]{2,1,0:T(8,128)(2,1)} %bitcast.80, bf16[2,64,1024]{2,1,0:T(8,128)(2,1)S(1)} %bitcast.75, bf16[2,1024,1024]{2,1,0:T(8,128)(2,1)} %bitcast.76), kind=kOutput, calls=%fused_computation.12 | convolution fusion | flops 537133056 | bytes 8912896 | tf_op jit(solution)/shard_map/mrn,mnc->mrc/dot_general | solution.py:79
  188.4 1.6 broadcast_in_dim.16.clone
  190.0 17.4 %while.1 = (s32[]{:T(128)}, bf16[2,32,16,1024]{3,2,0,1:T(8,128)(2,1)}, s32[2,4]{1,0:T(2,128)S(1)}, bf16[2,4,16,1024]{3,2,1,0:T(8,128)(2,1)S(1)}, s32[]{:T(128)}, /*index=5*/s32[4]{0:T(128)S(1)}) while((s32[]{:T(128)}, bf16[2,32,16,1024]{3,2,0,1:T(8,128)(2,1)}, s32[2,4]{1,0:T(2,128)S(1)}, bf16[2,4,16,1024]{3,2,1,0:T(8,128)(2,1)S(1)}, s32[]{:T(128)}, ...), condition=%wide.while_cond, body=%wide.while_body.sunk | while | flops 65565 | bytes 657586 | solution.py:84
  190.7 3.3 %and_reduce_fusion.2 = pred[]{:T(512)} fusion(s32[4]{0:T(128)S(1)} %get-tuple-element.91, s32[1]{0:T(128)} %bitcast.71, s32[1]{0:T(128)} %bitcast.72, s32[1]{0:T(128)} %bitcast.73, s32[1]{0:T(128)} %bitcast.74), kind=kLoop, calls=%fused_computation.3.clone.1 | loop fusion | flops 27 | bytes 33 | tf_op jit(solution)/shard_map/vmap(vmap())/scatter
  194.0 2.2 constant_dynamic-slice_fusion.6
  196.2 2.6 bitcast_dynamic-update-slice_fusion.2
  198.8 0.7 fusion.24
  199.4 3.3 %and_reduce_fusion.2 = pred[]{:T(512)} fusion(s32[4]{0:T(128)S(1)} %get-tuple-element.91, s32[1]{0:T(128)} %bitcast.71, s32[1]{0:T(128)} %bitcast.72, s32[1]{0:T(128)} %bitcast.73, s32[1]{0:T(128)} %bitcast.74), kind=kLoop, calls=%fused_computation.3.clone.1 | loop fusion | flops 27 | bytes 33 | tf_op jit(solution)/shard_map/vmap(vmap())/scatter
  202.7 2.2 constant_dynamic-slice_fusion.6
  204.9 2.6 bitcast_dynamic-update-slice_fusion.2
  207.5 9.8 %all-to-all-start.1 = ((bf16[32,2,16,1024]{3,2,1,0:T(8,128)(2,1)}), bf16[32,2,16,1024]{3,2,1,0:T(8,128)(2,1)S(1)}, u32[]{:S(2)}, u32[]{:S(2)}) async-start(bf16[32,2,16,1024]{3,2,1,0:T(8,128)(2,1)} %bitcast.10), calls=%async_computation.2 | async-start | bytes 4194304 | tf_op jit(solution)/shard_map/all_to_all | solution.py:89
  217.3 7.5 %copy.33 = bf16[2,4,256,1024]{2,1,3,0:T(4,128)(2,1)} copy(bf16[2,4,256,1024]{3,2,1,0:T(8,128)(2,1)} %all-gather.6.cloned.1.call-done) | data formatting | bytes 8388608 | tf_op jit(solution)/shard_map/all_gather | solution.py:60
  224.8 7.7 %reshape_reshape.7 = bf16[2,1024,4,16,16]{1,4,3,2,0:T(8,128)(2,1)} reshape(bf16[2,4,256,1024]{2,1,3,0:T(4,128)(2,1)} %copy.33) | data formatting | bytes 8388608 | tf_op jit(solution)/shard_map/reshape;reshape | solution.py:67
  232.6 1.1 constant_dynamic-slice_fusion.2
  233.7 3.5 %convolution_multiply_fusion = f32[2,64,1024]{2,1,0:T(8,128)S(1)} fusion(bf16[2,1024,64]{1,2,0:T(8,128)(2,1)S(1)} %bitcast.84, bf16[2,1024,1024]{2,1,0:T(8,128)(2,1)} %bitcast.77), kind=kOutput, calls=%fused_computation.9 | convolution fusion | flops 268566528 | bytes 4980736 | tf_op jit(solution)/shard_map/mnr,mnc->mrc/dot_general | solution.py:73
  237.2 0.9 add.53
  238.1 1.4 convolution_multiply_fusion.1
  239.5 0.9 add.51
  240.3 27.4 %all-to-all-done.1 = bf16[32,2,16,1024]{3,2,1,0:T(8,128)(2,1)S(1)} async-done(((bf16[32,2,16,1024]{3,2,1,0:T(8,128)(2,1)}), bf16[32,2,16,1024]{3,2,1,0:T(8,128)(2,1)S(1)}, u32[]{:S(2)}, u32[]{:S(2)}) %all-to-all-start.1) | async-done | bytes 2097184 | tf_op jit(solution)/shard_map/all_to_all | solution.py:89
  267.7 1.2 fusion.5
  268.9 0.7 reshape.118
  (31 shorter events, 1.2 us)
Async XLA Ops:
  7.2 176.2 %copy-start = (bf16[2,4,1,16,1024]{4,3,2,1,0:T(8,128)(2,1)S(1)}, bf16[2,4,1,16,1024]{4,3,2,1,0:T(8,128)(2,1)}, u32[]{:S(2)}) copy-start(bf16[2,4,1,16,1024]{4,3,2,1,0:T(8,128)(2,1)} %param.10) | copy-start | bytes 786436
  7.2 71.7 %reduce-scatter.2.cloned.1.call-start = ((), (), s32[]{:S(2)}) async-start(), calls=%async_computation.3 | async-start | bytes 2228224 | tf_op jit(solution)/shard_map/reduce_scatter | solution.py:32
  7.9 132.7 %all-gather.4.cloned.1.call-start = ((), (), s32[]{:S(2)}) async-start(), calls=%async_computation.4 | async-start | bytes 4456448 | tf_op jit(solution)/shard_map/all_gather | solution.py:29
  80.7 12.4 %copy-start.7 = (s32[32]{0:T(128)S(1)}, s32[32]{0:T(128)}, u32[]{:S(2)}) copy-start(s32[32]{0:T(128)} %param.7) | copy-start | bytes 388
  80.7 59.7 %copy-start.6 = (s32[3]{0:T(128)S(1)}, s32[3]{0:T(128)}, u32[]{:S(2)}) copy-start(s32[3]{0:T(128)} %constant.55.clone.1) | copy-start | bytes 40
  83.2 55.9 %all-to-all-start = ((bf16[32,2,16,1024]{3,2,1,0:T(8,128)(2,1)}), bf16[32,2,16,1024]{3,2,1,0:T(8,128)(2,1)S(1)}, u32[]{:S(2)}, u32[]{:S(2)}) async-start(bf16[32,2,16,1024]{3,2,1,0:T(8,128)(2,1)} %bitcast.3), calls=%async_computation.1 | async-start | bytes 4194304 | tf_op jit(solution)/shard_map/all_to_all | solution.py:54
  93.1 90.3 %all-gather.6.cloned.1.call-start = ((), (), s32[]{:S(2)}) async-start(), calls=%async_computation.5 | async-start | bytes 4456448 | tf_op jit(solution)/shard_map/all_gather | solution.py:60
  183.4 6.7 %copy-start.5 = (s32[4]{0:T(128)S(1)}, s32[4]{0:T(128)}, u32[]{:S(2)}) copy-start(s32[4]{0:T(128)} %constant.139) | copy-start | bytes 52
  207.5 60.3 %all-to-all-start.1 = ((bf16[32,2,16,1024]{3,2,1,0:T(8,128)(2,1)}), bf16[32,2,16,1024]{3,2,1,0:T(8,128)(2,1)S(1)}, u32[]{:S(2)}, u32[]{:S(2)}) async-start(bf16[32,2,16,1024]{3,2,1,0:T(8,128)(2,1)} %bitcast.10), calls=%async_computation.2 | async-start | bytes 4194304 | tf_op jit(solution)/shard_map/all_to_all | solution.py:89
  232.6 4.6 %copy-start.3 = (f32[2,4,1,16,1024]{4,3,2,1,0:T(8,128)S(1)}, f32[2,4,1,16,1024]{4,3,2,1,0:T(8,128)}, u32[]{:S(2)}) copy-start(f32[2,4,1,16,1024]{4,3,2,1,0:T(8,128)} %param.9) | copy-start | bytes 1572868
  232.6 5.5 %copy-start.1 = (bf16[2,4,256,1024]{3,2,1,0:T(8,128)(2,1)S(1)}, bf16[2,4,256,1024]{3,2,1,0:T(8,128)(2,1)}, u32[]{:S(2)}) copy-start(bf16[2,4,256,1024]{3,2,1,0:T(8,128)(2,1)} %all-gather.6.cloned.1.call-done) | copy-start | bytes 12582916
  232.6 5.5 %copy-start.2 = (bf16[2,4,16,1024]{3,2,1,0:T(8,128)(2,1)S(1)}, bf16[2,4,16,1024]{3,2,1,0:T(8,128)(2,1)}, u32[]{:S(2)}) copy-start(bf16[2,4,16,1024]{3,2,1,0:T(8,128)(2,1)} %gather_fusion) | copy-start | bytes 786436
  237.2 2.3 copy-start.4
Sparse Core Ops, SparseCore 0:
  10.8 68.0 reduce-scatter.1
  81.0 42.9 all-gather.3
  140.6 42.7 all-gather.5
where the time goes:
time: 277 us; the launch traced here: 276 us
  waiting for transfers between devices  187 us (68%)
  local copies, waits for them, and re-layouts  30.1 us (11%)
  starting transfers between devices  19.8 us (7%)
  between operations  13.9 us (5%)
  other arithmetic  13.7 us (5%)
  matrix products  12 us (4%)
    reduce_scatter x1, waiting for transfers between devices, on_device(): lax.psum_scatter(replica_grads[0].astype(jnp.float32).astype(jnp.bfloat16...  69.5 us
    all_to_all x1, waiting for transfers between devices, on_device(): lax.all_to_all(outgoing, 'fsdp', split_axis=0, concat_axis=0, tiled=True)  45.8 us
    all_gather x1, waiting for transfers between devices, on_device(): lax.all_gather(owned_rows, 'dp', axis=2, tiled=True)  42.7 us
    all_to_all x1, waiting for transfers between devices, on_device(): lax.all_to_all(homeward, 'fsdp', split_axis=0, concat_axis=0, tiled=True)  27.4 us
    scatter x4, other arithmetic  11.7 us
    all_to_all x1, starting transfers between devices, on_device(): lax.all_to_all(outgoing, 'fsdp', split_axis=0, concat_axis=0, tiled=True)  9.83 us
    all_to_all x1, starting transfers between devices, on_device(): lax.all_to_all(homeward, 'fsdp', split_axis=0, concat_axis=0, tiled=True)  9.82 us
    another operation x1, local copies, waits for them, and re-layouts, on_device(): entire.reshape(slots_here, block_size, sub_blocks, groups, strip_rows)  7.75 us
  transfers between devices with their start and end apart: 5, of which 4 were waited for; matrix products, arithmetic and copies ran while one was open for 11% of the time, Pallas kernels for 0%

commit v1 on v0

--- a/solution.py
+++ b/solution.py
@@ -2,6 +2,17 @@
 import jax.numpy as jnp
 from jax import lax
 from jax.sharding import PartitionSpec as P
+from jax.lax import all_to_all, axis_size
+
+
+def _rest_files(piece_in, axis_id):
+    step_out = all_to_all(
+        jnp.stack([piece_in for _ in range(axis_size(axis_id))]),
+        axis_id,
+        concat_axis=0,
+        split_axis=0,
+    )
+    return jnp.concatenate(step_out, axis=2)
 
 
 def on_device(
@@ -57,9 +68,7 @@
         in_axes=(1, 0),
     )(arrived, first_band)
     owned_rows = owned_rows.reshape(slots_here, sub_blocks, 1, strip_rows, block_size)
-    entire = lax.all_gather(owned_rows, "dp", axis=2, tiled=True).reshape(
-        slots_here, block_size, block_size
-    )
+    entire = _rest_files(owned_rows, "dp").reshape(slots_here, block_size, block_size)
     my_rows = owned_rows.reshape(slots_here, sub_blocks * strip_rows, block_size)
     left_gram = jnp.einsum("mrc,mnc->mrn", my_rows, entire, preferred_element_type=jnp.float32)
     left_new = left_gram_state + (left_gram / block_size).reshape(left_gram_state.shape)

time: 277 us -> 365 us (1.32)
  the two profiles are of different devices: /device:TPU:16 before, /device:TPU:2 now
where the time goes in v1:
time: 365 us; the launch traced here: 364 us
  waiting for transfers between devices  230 us (63%)
  local copies, waits for them, and re-layouts  70 us (19%)
  starting transfers between devices  24.6 us (7%)
  between operations  14.2 us (4%)
  other arithmetic  13.6 us (4%)
  matrix products  11.7 us (3%)
    all_to_all x1, waiting for transfers between devices, _rest_files(): all_to_all(jnp.stack([piece_in for _ in range(axis_size(axis_id))]), axis...  113 us
    reduce_scatter x1, waiting for transfers between devices, on_device(): lax.psum_scatter(replica_grads[0].astype(jnp.float32).astype(jnp.bfloat16...  70.4 us
    all_to_all x1, waiting for transfers between devices, on_device(): lax.all_to_all(outgoing, 'fsdp', split_axis=0, concat_axis=0, tiled=True)  45 us
    another operation x1, local copies, waits for them, and re-layouts, on_device(): entire.reshape(slots_here, block_size, sub_blocks, groups, strip_rows)  31.8 us
    dynamic_slice x2, local copies, waits for them, and re-layouts, on_device(): lax.dynamic_index_in_dim(entire.reshape(slots_here, block_size, sub_block...  17.7 us
    scatter x4, other arithmetic  11.5 us
    all_to_all x1, starting transfers between devices, on_device(): lax.all_to_all(outgoing, 'fsdp', split_axis=0, concat_axis=0, tiled=True)  9.86 us
    all_to_all x1, starting transfers between devices, on_device(): lax.all_to_all(homeward, 'fsdp', split_axis=0, concat_axis=0, tiled=True)  8.16 us
  transfers between devices with their start and end apart: 5, of which 3 were waited for; matrix products, arithmetic and copies ran while one was open for 17% of the time, Pallas kernels for 0%

profile of v1, /device:TPU:2, one launch (start us, length us, event | category | flops | bytes accessed | tf_op | source)
XLA Modules:
  0.0 363.8 jit_solution(12298872263226894064)
XLA Ops:
  7.2 0.7 reduce-scatter.2.cloned.1.call-update
  7.9 0.7 dynamic_slice.7
  8.7 70.4 %reduce-scatter.2.cloned.1.call-done = bf16[16,4096]{1,0:T(8,128)(2,1)} async-done(((bf16[256,4096]{1,0:T(8,128)(2,1)}), bf16[16,4096]{1,0:T(8,128)(2,1)}) %reduce-scatter.2.cloned.1.call-update) | async-done | bytes 131088 | tf_op jit(solution)/shard_map/reduce_scatter | solution.py:43
  79.1 1.0 reshape.109
  80.1 0.8 convolution_convert_fusion
  80.9 2.5 copy.39
  83.4 9.9 %all-to-all-start = ((bf16[32,2,16,1024]{3,2,1,0:T(8,128)(2,1)}), bf16[32,2,16,1024]{3,2,1,0:T(8,128)(2,1)S(1)}, u32[]{:S(2)}, u32[]{:S(2)}) async-start(bf16[32,2,16,1024]{3,2,1,0:T(8,128)(2,1)} %bitcast.3), calls=%async_computation.1 | async-start | bytes 4194304 | tf_op jit(solution)/shard_map/all_to_all | solution.py:65
  93.5 45.0 %all-to-all-done = bf16[32,2,16,1024]{3,2,1,0:T(8,128)(2,1)S(1)} async-done(((bf16[32,2,16,1024]{3,2,1,0:T(8,128)(2,1)}), bf16[32,2,16,1024]{3,2,1,0:T(8,128)(2,1)S(1)}, u32[]{:S(2)}, u32[]{:S(2)}) %all-to-all-start) | async-done | bytes 2097184 | tf_op jit(solution)/shard_map/all_to_all | solution.py:65
  139.0 2.5 stack.3
  141.5 6.5 %all-to-all-start.1 = ((bf16[16,2,4,1,16,1024]{5,4,2,1,3,0:T(8,128)(2,1)}), bf16[16,2,4,1,16,1024]{5,4,2,1,3,0:T(8,128)(2,1)}, u32[]{:S(2)}, u32[]{:S(2)}) async-start(bf16[16,2,4,1,16,1024]{5,4,2,1,3,0:T(8,128)(2,1)} %stack.3), calls=%async_computation.2 | async-start | bytes 8388608 | tf_op jit(solution)/shard_map/all_to_all | solution.py:9
  148.0 0.7 all-gather.2.cloned.1.call-update
  148.9 113.0 %all-to-all-done.1 = bf16[16,2,4,1,16,1024]{5,4,2,1,3,0:T(8,128)(2,1)} async-done(((bf16[16,2,4,1,16,1024]{5,4,2,1,3,0:T(8,128)(2,1)}), bf16[16,2,4,1,16,1024]{5,4,2,1,3,0:T(8,128)(2,1)}, u32[]{:S(2)}, u32[]{:S(2)}) %all-to-all-start.1) | async-done | bytes 4194336 | tf_op jit(solution)/shard_map/all_to_all | solution.py:9
  261.9 5.1 %copy.31 = bf16[2,4,16,1,16,1024]{5,4,2,1,0,3:T(8,128)(2,1)} copy(bf16[2,4,16,1,16,1024]{5,4,1,0,3,2:T(8,128)(2,1)} %bitcast.6) | data formatting | bytes 8388608 | tf_op jit(solution)/shard_map/reshape | solution.py:15
  267.0 5.1 %convolution_convert_fusion.2 = bf16[2,64,1024]{2,1,0:T(8,128)(2,1)S(1)} fusion(bf16[2,1024,1024]{2,1,0:T(8,128)(2,1)} %bitcast.83, bf16[2,64,1024]{2,1,0:T(8,128)(2,1)S(1)} %bitcast.78, bf16[2,1024,1024]{2,1,0:T(8,128)(2,1)} %bitcast.79), kind=kOutput, calls=%fused_computation.12 | convolution fusion | flops 537133056 | bytes 8912896 | tf_op jit(solution)/shard_map/mrn,mnc->mrc/dot_general | solution.py:88
  272.1 1.6 broadcast_in_dim.16.clone
  273.8 17.2 %while.1 = (s32[]{:T(128)}, bf16[2,32,16,1024]{3,2,0,1:T(8,128)(2,1)}, s32[2,4]{1,0:T(2,128)S(1)}, bf16[2,4,16,1024]{3,2,1,0:T(8,128)(2,1)S(1)}, s32[]{:T(128)}, /*index=5*/s32[4]{0:T(128)S(1)}) while((s32[]{:T(128)}, bf16[2,32,16,1024]{3,2,0,1:T(8,128)(2,1)}, s32[2,4]{1,0:T(2,128)S(1)}, bf16[2,4,16,1024]{3,2,1,0:T(8,128)(2,1)S(1)}, s32[]{:T(128)}, ...), condition=%wide.while_cond, body=%wide.while_body.sunk | while | flops 65565 | bytes 657586 | solution.py:93
  274.4 3.2 and_reduce_fusion.2
  277.6 2.2 constant_dynamic-slice_fusion.6
  279.8 2.5 bitcast_dynamic-update-slice_fusion.2
  283.0 3.2 and_reduce_fusion.2
  286.2 2.2 constant_dynamic-slice_fusion.6
  288.4 2.5 bitcast_dynamic-update-slice_fusion.2
  290.9 8.2 %all-to-all-start.2 = ((bf16[32,2,16,1024]{3,2,1,0:T(8,128)(2,1)}), bf16[32,2,16,1024]{3,2,1,0:T(8,128)(2,1)S(1)}, u32[]{:S(2)}, u32[]{:S(2)}) async-start(bf16[32,2,16,1024]{3,2,1,0:T(8,128)(2,1)} %bitcast.11), calls=%async_computation.3 | async-start | bytes 4194304 | tf_op jit(solution)/shard_map/all_to_all | solution.py:98
  299.1 31.8 %reshape_reshape_reshape.3 = bf16[2,1024,4,16,16]{4,3,2,1,0:T(8,128)(2,1)} reshape(bf16[2,4,16,1,16,1024]{5,4,2,1,0,3:T(8,128)(2,1)} %copy.31) | data formatting | bytes 8388608 | tf_op jit(solution)/shard_map/reshape;reshape;reshape | solution.py:76
  330.9 9.0 %constant_dynamic-slice_fusion.2 = bf16[2,1024,4,1,16]{4,3,2,1,0:T(2,128)(2,1)} fusion(bf16[2,1024,4,16,16]{4,3,2,1,0:T(8,128)(2,1)} %reshape_reshape_reshape.3, s32[]{:T(128)S(6)} %select_n.44), kind=kLoop, calls=%fused_computation.31 | loop fusion | bytes 524292 | tf_op jit(solution)/shard_map/jit(dynamic_index_in_dim)/dynamic_slice | solution.py:75
  340.0 8.7 %copy.37 = bf16[2,1024,4,1,16]{1,4,2,0,3:T(8,128)(2,1)S(1)} copy(bf16[2,1024,4,1,16]{4,3,2,1,0:T(2,128)(2,1)} %constant_dynamic-slice_fusion.2) | data formatting | bytes 524288 | tf_op jit(solution)/shard_map/jit(dynamic_index_in_dim)/dynamic_slice | solution.py:75
  348.6 3.2 convolution_multiply_fusion
  351.8 0.9 add.53
  352.7 1.4 convolution_multiply_fusion.1
  354.1 0.9 add.51
  355.0 1.2 fusion.5
  356.2 0.7 reshape.116
  (32 shorter events, 2.3 us)
Async XLA Ops:
  7.2 259.9 %copy-start = (bf16[2,4,1,16,1024]{4,3,2,1,0:T(8,128)(2,1)S(1)}, bf16[2,4,1,16,1024]{4,3,2,1,0:T(8,128)(2,1)}, u32[]{:S(2)}) copy-start(bf16[2,4,1,16,1024]{4,3,2,1,0:T(8,128)(2,1)} %param.10) | copy-start | bytes 786436
  7.2 71.9 %reduce-scatter.2.cloned.1.call-start = ((), (), s32[]{:S(2)}) async-start(), calls=%async_computation.4 | async-start | bytes 2228224 | tf_op jit(solution)/shard_map/reduce_scatter | solution.py:43
  80.9 12.4 %copy-start.7 = (s32[32]{0:T(128)S(1)}, s32[32]{0:T(128)}, u32[]{:S(2)}) copy-start(s32[32]{0:T(128)} %param.7) | copy-start | bytes 388
  83.4 55.1 %all-to-all-start = ((bf16[32,2,16,1024]{3,2,1,0:T(8,128)(2,1)}), bf16[32,2,16,1024]{3,2,1,0:T(8,128)(2,1)S(1)}, u32[]{:S(2)}, u32[]{:S(2)}) async-start(bf16[32,2,16,1024]{3,2,1,0:T(8,128)(2,1)} %bitcast.3), calls=%async_computation.1 | async-start | bytes 4194304 | tf_op jit(solution)/shard_map/all_to_all | solution.py:65
  141.5 7.2 %copy-start.6 = (s32[3]{0:T(128)S(1)}, s32[3]{0:T(128)}, u32[]{:S(2)}) copy-start(s32[3]{0:T(128)} %constant.55.clone.1) | copy-start | bytes 40
  141.5 120.4 %all-to-all-start.1 = ((bf16[16,2,4,1,16,1024]{5,4,2,1,3,0:T(8,128)(2,1)}), bf16[16,2,4,1,16,1024]{5,4,2,1,3,0:T(8,128)(2,1)}, u32[]{:S(2)}, u32[]{:S(2)}) async-start(bf16[16,2,4,1,16,1024]{5,4,2,1,3,0:T(8,128)(2,1)} %stack.3), calls=%async_computation.2 | async-start | bytes 8388608 | tf_op jit(solution)/shard_map/all_to_all | solution.py:9
  148.0 119.0 %all-gather.2.cloned.1.call-start = ((), (), s32[]{:S(2)}) async-start(), calls=%async_computation.5 | async-start | bytes 4456448 | tf_op jit(solution)/shard_map/all_gather | solution.py:40
  267.0 6.7 %copy-start.5 = (s32[4]{0:T(128)S(1)}, s32[4]{0:T(128)}, u32[]{:S(2)}) copy-start(s32[4]{0:T(128)} %constant.139) | copy-start | bytes 52
  290.9 64.0 %all-to-all-start.2 = ((bf16[32,2,16,1024]{3,2,1,0:T(8,128)(2,1)}), bf16[32,2,16,1024]{3,2,1,0:T(8,128)(2,1)S(1)}, u32[]{:S(2)}, u32[]{:S(2)}) async-start(bf16[32,2,16,1024]{3,2,1,0:T(8,128)(2,1)} %bitcast.11), calls=%async_computation.3 | async-start | bytes 4194304 | tf_op jit(solution)/shard_map/all_to_all | solution.py:98
  340.0 11.9 %copy-start.3 = (f32[2,4,1,16,1024]{4,3,2,1,0:T(8,128)S(1)}, f32[2,4,1,16,1024]{4,3,2,1,0:T(8,128)}, u32[]{:S(2)}) copy-start(f32[2,4,1,16,1024]{4,3,2,1,0:T(8,128)} %param.9) | copy-start | bytes 1572868
  348.6 4.1 %copy-start.2 = (bf16[2,4,16,1,16,1024]{5,4,2,1,0,3:T(8,128)(2,1)S(1)}, bf16[2,4,16,1,16,1024]{5,4,2,1,0,3:T(8,128)(2,1)}, u32[]{:S(2)}) copy-start(bf16[2,4,16,1,16,1024]{5,4,2,1,0,3:T(8,128)(2,1)} %copy.31) | copy-start | bytes 12582916
  351.8 2.3 copy-start.4
  352.7 4.2 %copy-start.1 = (bf16[2,4,1,16,1024]{4,3,2,1,0:T(8,128)(2,1)S(1)}, bf16[2,4,1,16,1024]{4,3,2,1,0:T(8,128)(2,1)}, u32[]{:S(2)}) copy-start(bf16[2,4,1,16,1024]{4,3,2,1,0:T(8,128)(2,1)} %param.10) | copy-start | bytes 786436
Sparse Core Ops, SparseCore 0:
  10.8 68.2 reduce-scatter.1
  151.0 97.5 all-gather.1
